TPU v7x, 256 devices: a whole 4x4x8 slice. The times are simulated.
256 devices in a mesh: pq: 8 (over z_hi, x), rs: 32 (over y, z_lo, core).
Axes of the slice: x: 4, y: 4, z: 8 (z_hi: 2, z_lo: 4; z = z_hi * 4 + z_lo), core: 2. Of those that a mesh axis runs over, the one named last changes fastest.
Arguments:
- integrals: bfloat16 [512, 1152, 1152], P('pq', 'rs'), may hold values from -6 to 6
- coeff: bfloat16 [1152, 896], P('rs', 'pq'), may hold values from -0.1875 to 0.1875
Outputs:
- half_mo: bfloat16 [512, 896, 896], P('pq', 'rs')
All inputs are finite; a program needn't handle non-finite values.
Results may differ from a plain program's by a relative error of at most 0.0049.
Values may be sent and summed in bfloat16 or wider, within the bound.
A program may use at most 128 MiB of HBM per device.

v0:
```python
import jax
import jax.numpy as jnp
from jax import lax
from jax.sharding import PartitionSpec as P

NBASIS = 1152
NORB = 896


def joined_along(parts, dim):
    parts = jnp.moveaxis(parts, 0, dim)
    lengths = parts.shape
    return parts.reshape(*lengths[:dim], lengths[dim] * lengths[dim + 1], *lengths[dim + 2 :])


def from_everyone(array, axis):
    count = lax.axis_size(axis)
    return lax.all_to_all(
        jnp.broadcast_to(array[None], (count, *array.shape)), axis, 0, 0, tiled=True
    )


def collect(array, axis, dim):
    return joined_along(from_everyone(array, axis), dim)


def second_half(received, panel):
    return jnp.einsum("prl,rk->plk", received, panel, preferred_element_type=jnp.float32).astype(
        jnp.bfloat16
    )


def on_device(integrals, coeff):
    pair_rows = integrals.shape[0]
    block_rows = integrals.shape[1]
    flat = integrals.reshape(pair_rows * block_rows, NBASIS)
    strip = collect(coeff, "pq", 1)
    panel = collect(strip, "rs", 0)
    first = jnp.dot(flat, panel, preferred_element_type=jnp.float32).astype(jnp.bfloat16)
    first = first.reshape(pair_rows, block_rows, NORB)
    return second_half(lax.all_to_all(first, "rs", split_axis=2, concat_axis=1, tiled=True), panel)


def solution(mesh):
    placed = (P("pq", "rs", None), P("rs", "pq"))
    return jax.shard_map(
        on_device, mesh=mesh, in_specs=placed, out_specs=P("pq", "rs", None), check_vma=False
    )
```

profile of v0, /device:TPU:1, one launch (start us, length us, event | category | flops | bytes accessed | tf_op | source)
XLA Modules:
  0.0 255.1 jit_solution(5755505084666371884)
XLA Ops:
  0.0 0.7 broadcast_in_dim.6
  0.7 20.4 %all_to_all.25 = bf16[8,36,112]{2,1,0:T(8,128)(2,1)S(1)} all-to-all(bf16[8,36,112]{2,1,0:T(8,128)(2,1)S(1)} %broadcast_in_dim.6), channel_id=1, replica_groups=mesh['pq'=8,'rs'=32] {'pq'}, dimensions={0} | all-to-all | bytes 129024 | tf_op jit(solution)/shard_map/all_to_all | solution.py:18
  21.1 0.1 broadcast_in_dim.14
  21.3 1.6 broadcast_in_dim.15
  22.8 8.1 %all-to-all-start.1 = ((bf16[32,36,896]{2,1,0:T(8,128)(2,1)}), bf16[32,36,896]{2,1,0:T(8,128)(2,1)S(1)}, u32[]{:S(2)}, u32[]{:S(2)}) async-start(bf16[32,36,896]{2,1,0:T(8,128)(2,1)} %broadcast_in_dim.15), calls=%async_computation.1 | async-start | bytes 4587520 | tf_op jit(solution)/shard_map/all_to_all | solution.py:18
  30.9 8.0 %copy.15 = bf16[64,36,1152]{2,1,0:T(8,128)(2,1)} copy(bf16[64,36,1152]{2,0,1:T(8,128)(2,1)} %param.2) | data formatting | bytes 10616832 | tf_op args[0]
  39.0 8.9 %reshape.11 = bf16[2304,1152]{1,0:T(8,128)(2,1)} reshape(bf16[64,36,1152]{2,1,0:T(8,128)(2,1)} %copy.15) | data formatting | bytes 10616832 | tf_op jit(solution)/shard_map/reshape | solution.py:36
  47.8 37.1 %all-to-all-done.1 = bf16[32,36,896]{2,1,0:T(8,128)(2,1)S(1)} async-done(((bf16[32,36,896]{2,1,0:T(8,128)(2,1)}), bf16[32,36,896]{2,1,0:T(8,128)(2,1)S(1)}, u32[]{:S(2)}, u32[]{:S(2)}) %all-to-all-start.1) | async-done | bytes 2064416 | tf_op jit(solution)/shard_map/all_to_all | solution.py:18
  84.9 1.9 reshape.12
  86.9 10.0 %convolution_convert_fusion = bf16[2304,896]{1,0:T(8,128)(2,1)} fusion(bf16[2304,1152]{1,0:T(8,128)(2,1)} %reshape.11, bf16[1152,896]{1,0:T(8,128)(2,1)} %reshape.12), kind=kOutput, calls=%fused_computation.4 | convolution fusion | flops 4758405120 | bytes 11501568 | tf_op jit(solution)/shard_map/dot_general | solution.py:39
  96.8 6.9 %reshape.13 = bf16[64,36,896]{2,1,0:T(8,128)(2,1)} reshape(bf16[2304,896]{1,0:T(8,128)(2,1)} %convolution_convert_fusion) | data formatting | bytes 8257536 | tf_op jit(solution)/shard_map/reshape | solution.py:40
  103.7 13.9 %copy.17 = bf16[64,36,896]{0,1,2:T(8,128)(2,1)} copy(bf16[64,36,896]{2,1,0:T(8,128)(2,1)} %reshape.13) | data formatting | bytes 8257536 | tf_op jit(solution)/shard_map/reshape | solution.py:40
  117.6 13.7 %reshape.16 = bf16[32,2,32256]{2,1,0:T(2,128)(2,1)} reshape(bf16[896,36,64]{2,1,0:T(8,128)(2,1)} %bitcast.18) | data formatting | bytes 8257536
  131.3 99.3 %all_to_all.26 = bf16[32,2,32256]{2,1,0:T(2,128)(2,1)} all-to-all(bf16[32,2,32256]{2,1,0:T(2,128)(2,1)} %reshape.16), channel_id=1, replica_groups=mesh['pq'=8,'rs'=32] {'rs'}, dimensions={0} | all-to-all | bytes 8257536 | tf_op jit(solution)/shard_map/all_to_all | solution.py:41
  230.6 14.6 %reshape.17 = bf16[896,36,64]{2,1,0:T(8,128)(2,1)} reshape(bf16[32,2,32256]{2,1,0:T(2,128)(2,1)} %all_to_all.26) | data formatting | bytes 8257536
  245.2 9.9 %bitcast_convert_fusion = bf16[64,28,896]{2,0,1:T(8,128)(2,1)} fusion(bf16[64,36,32,28]{0,1,3,2:T(8,128)(2,1)} %bitcast.17, bf16[32,36,896]{2,1,0:T(8,128)(2,1)S(1)} %all-to-all-done.1), kind=kOutput, calls=%fused_computation.3 | convolution fusion | flops 3700981760 | bytes 9404416 | tf_op jit(solution)/shard_map/prl,rk->plk/dot_general | solution.py:28
  (1 shorter events, 0.0 us)
Async XLA Ops:
  22.8 62.1 %all-to-all-start.1 = ((bf16[32,36,896]{2,1,0:T(8,128)(2,1)}), bf16[32,36,896]{2,1,0:T(8,128)(2,1)S(1)}, u32[]{:S(2)}, u32[]{:S(2)}) async-start(bf16[32,36,896]{2,1,0:T(8,128)(2,1)} %broadcast_in_dim.15), calls=%async_computation.1 | async-start | bytes 4587520 | tf_op jit(solution)/shard_map/all_to_all | solution.py:18
where the time goes:
time: 257 us; the launch traced here: 255 us
  blocking collectives  120 us (47%)
  local copies, waits for them, and re-layouts  70.4 us (27%)
  waiting for transfers between devices  37.1 us (14%)
  matrix products  19.8 us (8%)
  starting transfers between devices  8.09 us (3%)
    all_to_all x1, blocking collectives, on_device(): lax.all_to_all(first, 'rs', split_axis=2, concat_axis=1, tiled=True)  99.3 us
    all_to_all x1, waiting for transfers between devices, from_everyone(): lax.all_to_all(jnp.broadcast_to(array[None], (count, *array.shape)), axis...  37.1 us
    unnamed x3, local copies, waits for them, and re-layouts  36.4 us
    reshape x2, local copies, waits for them, and re-layouts, on_device(): first = first.reshape(pair_rows, block_rows, NORB)  20.8 us
    all_to_all x1, blocking collectives, from_everyone(): lax.all_to_all(jnp.broadcast_to(array[None], (count, *array.shape)), axis...  20.4 us
    dot_general x1, matrix products, on_device(): jnp.dot(flat, panel, preferred_element_type=jnp.float32)  9.95 us
    dot_general x1, matrix products, second_half(): jnp.einsum('prl,rk->plk', received, panel, preferred_element_type=jnp.flo...  9.88 us
    reshape x1, local copies, waits for them, and re-layouts, on_device(): flat = integrals.reshape(pair_rows * block_rows, NBASIS)  8.88 us
  transfers between devices with their start and end apart: 1, of which 1 were waited for; matrix products, arithmetic and copies ran while one was open for 7% of the time, Pallas kernels for 0%

commit v1 on v0

v1 whole, which is shorter than its diff:
```python
import functools
import jax
import jax.numpy as jnp
from jax import lax
from jax.experimental import pallas as pl
from jax.experimental.pallas import tpu as pltpu
from jax.sharding import PartitionSpec as P

MESH = pl.DeviceIdType.MESH
BF16 = jnp.bfloat16
F32 = jnp.float32


def swapped(tile):
    rows = lax.broadcasted_iota(jnp.int32, tile.shape, 0) % 2
    lanes = lax.broadcasted_iota(jnp.int32, tile.shape, 1) // 64
    turned = pltpu.roll(tile, 64, 1)
    above = pltpu.roll(turned, tile.shape[0] - 1, 0)
    below = pltpu.roll(turned, 1, 0)
    return jnp.where(rows == lanes, tile, jnp.where(rows == 0, above, below))


def kernel(i_hbm, pt_hbm, c_hbm, o_hbm, i_v, pt_v, c_v, s_v, r_v, o_v, in_sems, out_sems, send_sems, recv_sems):
    me = lax.axis_index("rs")
    loads = [
        pltpu.make_async_copy(src, dst, in_sems.at[n])
        for n, (src, dst) in enumerate(((i_hbm, i_v), (pt_hbm, pt_v), (c_hbm, c_v)))
    ]
    for load in loads:
        load.start()
    barrier = pltpu.get_barrier_semaphore()

    def greet(k, _):
        pl.semaphore_signal(barrier, inc=1, device_id={"rs": lax.rem(me + k, 32)}, device_id_type=MESH)
        return 0

    lax.fori_loop(1, 32, greet, 0)
    loads[0].wait()
    loads[1].wait()
    pl.semaphore_wait(barrier, 31)

    def send(q, d):
        return pltpu.make_async_remote_copy(
            src_ref=s_v.at[q, d],
            dst_ref=r_v.at[q, :, me],
            send_sem=send_sems.at[q],
            recv_sem=recv_sems.at[q],
            device_id={"rs": d},
            device_id_type=MESH,
        )

    def first(q, _):
        def columns(g, _):
            acc = lax.dot_general(
                pt_v[q], i_v[pl.ds(pl.multiple_of(g * 256, 256), 256), :], (((1,), (1,)), ((), ())), preferred_element_type=F32
            )
            for h in range(2):
                tile = swapped(acc[:, h * 128 : (h + 1) * 128]).astype(BF16)
                s_v[q, :, :, 2 * g + h] = tile.reshape(32, 2, 2, 128)
            return 0

        lax.fori_loop(0, 9, columns, 0)

        def issue(k, _):
            send(q, lax.rem(me + k, 32)).start()
            return 0

        lax.fori_loop(1, 32, issue, 0)
        r_v[q, :, me] = s_v[q, me]
        return 0

    lax.fori_loop(0, 7, first, 0)
    loads[2].wait()

    def second(q, _):
        pltpu.make_async_copy(r_v.at[q, :, pl.ds(0, 31)], r_v.at[q, :, pl.ds(0, 31)], recv_sems.at[q]).wait()
        for lp in range(2):
            x = r_v[q, lp].reshape(1152, 128)
            acc = lax.dot_general(x, c_v[...], (((0,), (0,)), ((), ())), preferred_element_type=F32)
            o_v[q, pl.ds(lp * 128, 128), :] = acc.astype(BF16)
        pltpu.make_async_copy(o_v.at[q], o_hbm.at[q], out_sems.at[q]).start()
        return 0

    lax.fori_loop(0, 7, second, 0)

    def drain(q, _):
        pltpu.make_async_copy(o_v.at[q], o_hbm.at[q], out_sems.at[q]).wait()
        pltpu.make_async_copy(s_v.at[q, pl.ds(0, 31)], s_v.at[q, pl.ds(0, 31)], send_sems.at[q]).wait()
        return 0

    lax.fori_loop(0, 7, drain, 0)


def transform(i2d, pt, c):
    any_ = pl.BlockSpec(memory_space=pl.ANY)
    return pl.pallas_call(
        kernel,
        out_shape=jax.ShapeDtypeStruct((7, 256, 896), BF16),
        in_specs=[any_] * 3,
        out_specs=any_,
        scratch_shapes=[
            pltpu.VMEM((2304, 1152), BF16),
            pltpu.VMEM((7, 128, 1152), BF16),
            pltpu.VMEM((1152, 896), BF16),
            pltpu.VMEM((7, 32, 2, 18, 2, 128), BF16),
            pltpu.VMEM((7, 2, 32, 18, 2, 128), BF16),
            pltpu.VMEM((7, 256, 896), BF16),
            pltpu.SemaphoreType.DMA((3,)),
            pltpu.SemaphoreType.DMA((7,)),
            pltpu.SemaphoreType.DMA((7,)),
            pltpu.SemaphoreType.DMA((7,)),
        ],
        compiler_params=pltpu.CompilerParams(collective_id=0, has_side_effects=True, vmem_limit_bytes=60 * 2**20),
        name="half",
    )(i2d, pt, c)


def on_device(integrals, coeff):
    i2d = integrals.transpose(1, 0, 2).reshape(2304, 1152)
    strip = lax.all_gather(coeff, "pq", axis=1, tiled=True)
    panel = lax.all_gather(strip, "rs", axis=0, tiled=True)
    pt = panel.T.reshape(32, 7, 4, 1152).transpose(1, 0, 2, 3).reshape(7, 128, 1152)
    out = transform(i2d, pt, panel)
    return out.reshape(28, 64, 896).transpose(1, 0, 2)


def solution(mesh):
    placed = (P("pq", "rs", None), P("rs", "pq"))
    return jax.shard_map(on_device, mesh=mesh, in_specs=placed, out_specs=P("pq", "rs", None), check_vma=False)
```

time: 257 us -> 239 us (0.930)
  Pallas kernels: 0 us -> 99.4 us
  blocking collectives: 120 us -> 40.6 us
  local copies, waits for them, and re-layouts: 70.4 us -> 18.1 us
  waiting for transfers between devices: 37.1 us -> 67.4 us
  matrix products: 19.8 us -> 0 us
  between operations: 0.02 us -> 13.4 us
  starting transfers between devices: 8.09 us -> 0.01 us
    all_to_all x2 -> x0, blocking collectives: 120 us -> none  [the longest x1 99.3 us: on_device(): lax.all_to_all(first, 'rs', split_axis=2, concat_axis=1, tiled=True)]
    pallas_call x0 -> x1, Pallas kernels: none -> 99.4 us  [transform(): pl.pallas_call(kernel, out_shape=jax.ShapeDtypeStruct((7, 256, 896), BF16...]
    all_gather x0 -> x1, waiting for transfers between devices: none -> 67.3 us  [on_device(): panel = lax.all_gather(strip, 'rs', axis=0, tiled=True)]
    all_gather x0 -> x1, blocking collectives: none -> 40.6 us  [on_device(): strip = lax.all_gather(coeff, 'pq', axis=1, tiled=True)]
    all_to_all x1 -> x0, waiting for transfers between devices: 37.1 us -> none  [from_everyone(): lax.all_to_all(jnp.broadcast_to(array[None], (count, *array.shape)), axis...]
    unnamed x3 -> x5, local copies, waits for them, and re-layouts: 36.4 us -> 7.16 us
    reshape x4 -> x2, local copies, waits for them, and re-layouts: 31.6 us -> 5.97 us  [on_device(): panel.T.reshape(32, 7, 4, 1152).transpose(1, 0, 2, 3).reshape(7, 128, 1152)]
    dot_general x2 -> x0, matrix products: 19.8 us -> none  [the longest x1 9.95 us: on_device(): jnp.dot(flat, panel, preferred_element_type=jnp.float32)]
  transfers between devices with their start and end apart: 1 -> 1, of which waited for: 1 -> 1; matrix products, arithmetic and copies ran while one was open for 7% -> 0% of each run, Pallas kernels for 0% -> 0%
where the time goes in v1:
time: 239 us
  Pallas kernels  99.4 us (42%)
  waiting for transfers between devices  67.4 us (28%)
  blocking collectives  40.6 us (17%)
  local copies, waits for them, and re-layouts  18.1 us (8%)
  between operations  13.4 us (6%)
    pallas_call x1, Pallas kernels, transform(): pl.pallas_call(kernel, out_shape=jax.ShapeDtypeStruct((7, 256, 896), BF16...  99.4 us
    all_gather x1, waiting for transfers between devices, on_device(): panel = lax.all_gather(strip, 'rs', axis=0, tiled=True)  67.3 us
    all_gather x1, blocking collectives, on_device(): strip = lax.all_gather(coeff, 'pq', axis=1, tiled=True)  40.6 us
    unnamed x5, local copies, waits for them, and re-layouts  7.16 us
    reshape x2, local copies, waits for them, and re-layouts, on_device(): panel.T.reshape(32, 7, 4, 1152).transpose(1, 0, 2, 3).reshape(7, 128, 1152)  5.97 us
    transpose x2, local copies, waits for them, and re-layouts, on_device(): panel.T.reshape(32, 7, 4, 1152).transpose(1, 0, 2, 3).reshape(7, 128, 1152)  4.92 us
  transfers between devices with their start and end apart: 1, of which 1 were waited for; matrix products, arithmetic and copies ran while one was open for 0% of the time, Pallas kernels for 0%

profile of v1, /device:TPU:1, one launch (start us, length us, event | category | flops | bytes accessed | tf_op | source)
XLA Modules:
  0.0 239.0 jit_solution(10796748041399724764)
XLA Ops:
  6.5 0.0 all-gather.4.cloned.1.call-start
  6.5 40.6 %all-gather = bf16[8,112,36]{1,2,0:T(8,128)(2,1)S(1)} all-gather(bf16[1,112,36]{1,2,0:T(8,128)(2,1)} %bitcast.21), channel_id=1, replica_groups=mesh['pq'=8,'rs'=32] {'pq'}, dimensions={0}, use_global_device_ids=true | all-gather | bytes 72576 | tf_op jit(solution)/shard_map/all_gather | solution.py:120
  47.2 0.8 reshape.17
  48.0 0.0 all-gather.4.cloned.1.call-update
  48.0 67.3 %all-gather.4.cloned.1.call-done = bf16[32,36,896]{2,1,0:T(8,128)(2,1)} async-done(((bf16[1,36,896]{2,1,0:T(8,128)(2,1)}), bf16[32,36,896]{2,1,0:T(8,128)(2,1)}) %all-gather.4.cloned.1.call-update) | async-done | bytes 2064400 | tf_op jit(solution)/shard_map/all_gather | solution.py:121
  115.3 2.5 %reshape.19.c_hbm = bf16[1152,896]{1,0:T(8,128)(2,1)S(1)} reshape(bf16[32,36,896]{2,1,0:T(8,128)(2,1)} %all-gather.4.cloned.1.call-done) | data formatting | bytes 4128768
  117.9 0.0 copy-start
  117.9 2.6 %copy.8 = bf16[896,1152]{1,0:T(8,128)(2,1)} copy(bf16[896,1152]{0,1:T(8,128)(2,1)S(1)} %bitcast.16) | data formatting | bytes 4128768 | tf_op jit(solution)/shard_map/transpose | solution.py:122
  120.5 0.0 copy-done
  120.5 4.4 %reshape.13 = bf16[32,7,4,1152]{3,2,1,0:T(4,128)(2,1)} reshape(bf16[896,1152]{1,0:T(8,128)(2,1)} %copy.8) | data formatting | bytes 4128768 | tf_op jit(solution)/shard_map/reshape | solution.py:122
  125.0 2.3 copy.9
  127.2 1.6 reshape.14.pt_hbm
  128.8 99.4 %half.1 = bf16[7,256,896]{2,1,0:T(8,128)(2,1)} custom-call(bf16[2304,1152]{1,0:T(8,128)(2,1)} %bitcast.19, bf16[7,128,1152]{2,1,0:T(8,128)(2,1)} %reshape.14.pt_hbm, bf16[1152,896]{1,0:T(8,128)(2,1)} %copy-done), custom_call_target="tpu_custom_call" | custom-call | tf_op jit(solution)/shard_map/half/pallas_call | solution.py:96
  228.2 3.9 %copy.11 = bf16[64,28,896]{2,0,1:T(8,128)(2,1)} copy(bf16[64,28,896]{2,0,1:T(8,128)(2,1)} %bitcast.17) | data formatting | bytes 6422528
  (1 shorter events, 0.0 us)
Async XLA Ops:
  6.5 108.8 %all-gather.4.cloned.1.call-start = ((), (), s32[]{:S(2)}) async-start(), calls=%async_computation | async-start | bytes 2365440 | tf_op jit(solution)/shard_map/all_gather | solution.py:121
  117.9 2.6 %copy-start = (bf16[1152,896]{1,0:T(8,128)(2,1)}, bf16[1152,896]{1,0:T(8,128)(2,1)S(1)}, u32[]{:S(2)}) copy-start(bf16[1152,896]{1,0:T(8,128)(2,1)S(1)} %reshape.19.c_hbm) | copy-start | bytes 6193156
Sparse Core Ops, SparseCore 0:
  48.1 67.1 all-gather.3

commit v2 on v1

v2 whole, which is shorter than its diff:
```python
import jax
import jax.numpy as jnp
from jax import lax
from jax.experimental import pallas as pl
from jax.experimental.pallas import tpu as pltpu
from jax.sharding import PartitionSpec as P

MESH = pl.DeviceIdType.MESH
BF16 = jnp.bfloat16
F32 = jnp.float32
CHUNKS = 7


def one_hot(shape, column_of_row):
    rows = lax.broadcasted_iota(jnp.int32, shape, 0)
    columns = lax.broadcasted_iota(jnp.int32, shape, 1)
    return jnp.where(column_of_row(rows) == columns, 1.0, 0.0).astype(BF16)


def swapped(tile):
    rows = lax.broadcasted_iota(jnp.int32, tile.shape, 0) % 2
    lanes = lax.broadcasted_iota(jnp.int32, tile.shape, 1) // 64
    turned = pltpu.roll(tile, 64, 1)
    above = pltpu.roll(turned, tile.shape[0] - 1, 0)
    below = pltpu.roll(turned, 1, 0)
    return jnp.where(rows == lanes, tile, jnp.where(rows == 0, above, below))


def kernel(
    i_hbm, b_hbm, o_hbm,
    i_v, blk_v, b_v, z_v, at_v, g_v, pt_v, perm_v, c_v, s_v, r_v, o_v,
    in_sems, out_sems, zsend, zrecv, gsend, grecv, send_sems, recv_sems,
):
    pq, rs = lax.axis_index("pq"), lax.axis_index("rs")
    zh, x = pq // 4, pq % 4
    y, zl, core = rs // 8, (rs // 2) % 4, rs % 2
    z = zh * 4 + zl

    def column_peer(k):
        pz, pc = (z + k // 2) % 8, (core + k) % 2
        return {"pq": (pz // 4) * 4 + x, "rs": y * 8 + (pz % 4) * 2 + pc}

    def plane_peer(k):
        py, px = (y + k // 4) % 4, (x + k) % 4
        return {"pq": zh * 4 + px, "rs": py * 8 + zl * 2 + core}

    def row_peer(k):
        return {"rs": (rs + k) % 32}

    load_i = pltpu.make_async_copy(i_hbm, i_v, in_sems.at[0])
    load_b = pltpu.make_async_copy(b_hbm, blk_v, in_sems.at[1])
    load_b.start()
    load_i.start()
    barrier = pltpu.get_barrier_semaphore()

    def greet(peer):
        def one(k, _):
            pl.semaphore_signal(barrier, inc=1, device_id=peer(k), device_id_type=MESH)
            return 0

        return one

    z_v[...] = jnp.zeros(z_v.shape, BF16)
    b_v[...] = jnp.zeros(b_v.shape, BF16)
    lax.fori_loop(1, 16, greet(column_peer), 0)
    lax.fori_loop(1, 16, greet(plane_peer), 0)
    lax.fori_loop(1, 32, greet(row_peer), 0)

    load_b.wait()
    b_v[:, :, 0:112] = blk_v[...].reshape(9, 4, 112)
    spot = zh * 96 + y * 8 + (zl * 2 + core) * 9
    z_v[pl.ds(spot, 9)] = b_v[...]
    pl.semaphore_wait(barrier, 61)

    def send_block(k, _):
        pltpu.make_async_remote_copy(
            src_ref=b_v, dst_ref=z_v.at[pl.ds(spot, 9)], send_sem=zsend, recv_sem=zrecv,
            device_id=column_peer(k), device_id_type=MESH,
        ).start()
        return 0

    lax.fori_loop(1, 16, send_block, 0)
    order = one_hot((128, 128), lambda n: jnp.where(n < 112, ((n // 4) % 4) * 28 + (n // 16) * 4 + n % 4, -1))
    perm_v[...] = one_hot(
        perm_v.shape, lambda n: ((n // 16) % 8) * 112 + ((n // 4) % 4) * 28 + (n // 128) * 4 + n % 4
    )
    pltpu.make_async_copy(z_v.at[pl.ds(0, 135)], z_v.at[pl.ds(0, 135)], zrecv).wait()
    mine = y * 4 + x
    for h in range(2):
        strip = z_v[pl.ds(h * 96, 96)].reshape(384, 128)
        turned = lax.dot_general(order, strip, (((1,), (1,)), ((), ())), preferred_element_type=F32).astype(BF16)
        for q in range(CHUNKS):
            at_v[q, h] = turned[q * 16 : (q + 1) * 16]
            g_v[q, mine, h] = turned[q * 16 : (q + 1) * 16]

    def spread(q):
        def one(k, _):
            pltpu.make_async_remote_copy(
                src_ref=at_v.at[q], dst_ref=g_v.at[q, mine], send_sem=gsend.at[q], recv_sem=grecv.at[q],
                device_id=plane_peer(k), device_id_type=MESH,
            ).start()
            return 0

        lax.fori_loop(1, 16, one, 0)

    spread(0)
    spread(1)
    load_i.wait()

    def first(q, _):
        pltpu.make_async_copy(g_v.at[q, pl.ds(0, 15)], g_v.at[q, pl.ds(0, 15)], grecv.at[q]).wait()
        rows = pl.ds(pl.multiple_of(q * 128, 128), 128)
        windows = [
            jnp.concatenate([g_v[q, w * 4 + px, h] for h in range(2) for px in range(4)], axis=0) for w in range(4)
        ]
        for t in range(9):
            parts = [windows[w][:, (t - 2 * w) * 128 : (t - 2 * w + 1) * 128] for w in range(4) if 0 <= t - 2 * w < 3]
            pt_v[rows, t * 128 : (t + 1) * 128] = sum(parts[1:], parts[0])

        def columns(g, _):
            acc = lax.dot_general(
                pt_v[rows, :], i_v[pl.ds(pl.multiple_of(g * 256, 256), 256), :], (((1,), (1,)), ((), ())),
                preferred_element_type=F32,
            )
            for h in range(2):
                tile = swapped(acc[:, h * 128 : (h + 1) * 128]).astype(BF16)
                s_v[q, :, :, 2 * g + h] = tile.reshape(32, 2, 2, 128)
            return 0

        lax.fori_loop(0, 9, columns, 0)

        def issue(k, _):
            d = (rs + k) % 32
            pltpu.make_async_remote_copy(
                src_ref=s_v.at[q, d], dst_ref=r_v.at[q, :, rs], send_sem=send_sems.at[q], recv_sem=recv_sems.at[q],
                device_id={"rs": d}, device_id_type=MESH,
            ).start()
            return 0

        lax.fori_loop(1, 32, issue, 0)
        r_v[q, :, rs] = s_v[q, rs]

        @pl.when(q < CHUNKS - 2)
        def _():
            spread(q + 2)

        return 0

    lax.fori_loop(0, CHUNKS, first, 0)

    def natural(g, _):
        rows = pl.ds(pl.multiple_of(g * 128, 128), 128)
        acc = lax.dot_general(pt_v[:, rows], perm_v[...], (((0,), (0,)), ((), ())), preferred_element_type=F32)
        c_v[rows, :] = acc.astype(BF16)
        return 0

    lax.fori_loop(0, 9, natural, 0)

    def second(q, _):
        pltpu.make_async_copy(r_v.at[q, :, pl.ds(0, 31)], r_v.at[q, :, pl.ds(0, 31)], recv_sems.at[q]).wait()
        for lp in range(2):
            tiles = r_v[q, lp].reshape(NBASIS, 128)
            acc = lax.dot_general(tiles, c_v[...], (((0,), (0,)), ((), ())), preferred_element_type=F32)
            o_v[q, pl.ds(lp * 128, 128), :] = acc.astype(BF16)
        pltpu.make_async_copy(o_v.at[q], o_hbm.at[q], out_sems.at[q]).start()
        return 0

    lax.fori_loop(0, CHUNKS, second, 0)

    def drain(q, _):
        pltpu.make_async_copy(o_v.at[q], o_hbm.at[q], out_sems.at[q]).wait()
        pltpu.make_async_copy(s_v.at[q, pl.ds(0, 31)], s_v.at[q, pl.ds(0, 31)], send_sems.at[q]).wait()
        pltpu.make_async_copy(g_v.at[q, pl.ds(0, 15)], g_v.at[q, pl.ds(0, 15)], gsend.at[q]).wait()
        return 0

    lax.fori_loop(0, CHUNKS, drain, 0)
    pltpu.make_async_copy(z_v.at[pl.ds(0, 135)], z_v.at[pl.ds(0, 135)], zsend).wait()


NBASIS = 1152
NORB = 896


def transform(flat, block):
    anywhere = pl.BlockSpec(memory_space=pl.ANY)
    dma = pltpu.SemaphoreType.DMA
    return pl.pallas_call(
        kernel,
        out_shape=jax.ShapeDtypeStruct((CHUNKS, 256, NORB), BF16),
        in_specs=[anywhere] * 2,
        out_specs=anywhere,
        scratch_shapes=[
            pltpu.VMEM((2304, NBASIS), BF16),
            pltpu.VMEM((36, 112), BF16),
            pltpu.VMEM((9, 4, 128), BF16),
            pltpu.VMEM((192, 4, 128), BF16),
            pltpu.VMEM((CHUNKS, 2, 16, 384), BF16),
            pltpu.VMEM((CHUNKS, 16, 2, 16, 384), BF16),
            pltpu.VMEM((NORB, NBASIS), BF16),
            pltpu.VMEM((NORB, NORB), BF16),
            pltpu.VMEM((NBASIS, NORB), BF16),
            pltpu.VMEM((CHUNKS, 32, 2, 18, 2, 128), BF16),
            pltpu.VMEM((CHUNKS, 2, 32, 18, 2, 128), BF16),
            pltpu.VMEM((CHUNKS, 256, NORB), BF16),
            dma((2,)),
            dma((CHUNKS,)),
            dma,
            dma,
            dma((CHUNKS,)),
            dma((CHUNKS,)),
            dma((CHUNKS,)),
            dma((CHUNKS,)),
        ],
        compiler_params=pltpu.CompilerParams(collective_id=0, has_side_effects=True, vmem_limit_bytes=60 * 2**20),
        name="half",
    )(flat, block)


def on_device(integrals, coeff):
    flat = integrals.transpose(1, 0, 2).reshape(2304, NBASIS)
    return transform(flat, coeff).reshape(28, 64, NORB).transpose(1, 0, 2)


def solution(mesh):
    placed = (P("pq", "rs", None), P("rs", "pq"))
    return jax.shard_map(on_device, mesh=mesh, in_specs=placed, out_specs=P("pq", "rs", None), check_vma=False)
```

time: 239 us -> 126 us (0.53)
  waiting for transfers between devices: 67.4 us -> 0 us
  blocking collectives: 40.6 us -> 0 us
  Pallas kernels: 99.4 us -> 122 us
  local copies, waits for them, and re-layouts: 18.1 us -> 3.86 us
  between operations: 13.4 us -> 0.01 us
    all_gather x1 -> x0, waiting for transfers between devices: 67.3 us -> none  [on_device(): panel = lax.all_gather(strip, 'rs', axis=0, tiled=True)]
    all_gather x1 -> x0, blocking collectives: 40.6 us -> none  [on_device(): strip = lax.all_gather(coeff, 'pq', axis=1, tiled=True)]
    pallas_call x1, Pallas kernels: 99.4 us -> 122 us  [transform(): pl.pallas_call(kernel, out_shape=jax.ShapeDtypeStruct((CHUNKS, 256, NORB)...]
    reshape x2 -> x0, local copies, waits for them, and re-layouts: 5.97 us -> none  [on_device(): panel.T.reshape(32, 7, 4, 1152).transpose(1, 0, 2, 3).reshape(7, 128, 1152)]
    transpose x2 -> x0, local copies, waits for them, and re-layouts: 4.92 us -> none  [on_device(): panel.T.reshape(32, 7, 4, 1152).transpose(1, 0, 2, 3).reshape(7, 128, 1152)]
    unnamed x5 -> x1, local copies, waits for them, and re-layouts: 7.16 us -> 3.86 us
  transfers between devices with their start and end apart: 1 -> 0, of which waited for: 1 -> 0; matrix products, arithmetic and copies ran while one was open for 0% -> 0% of each run, Pallas kernels for 0% -> 0%
where the time goes in v2:
time: 126 us; the launch traced here: 125 us
  Pallas kernels  122 us (97%)
  local copies, waits for them, and re-layouts  3.86 us (3%)
    pallas_call x1, Pallas kernels, transform(): pl.pallas_call(kernel, out_shape=jax.ShapeDtypeStruct((CHUNKS, 256, NORB)...  122 us
    unnamed x1, local copies, waits for them, and re-layouts  3.86 us

profile of v2, /device:TPU:1, one launch (start us, length us, event | category | flops | bytes accessed | tf_op | source)
XLA Modules:
  0.0 125.5 jit_solution(13819099472003130554)
XLA Ops:
  0.0 121.6 %half.1 = bf16[7,256,896]{2,1,0:T(8,128)(2,1)} custom-call(bf16[2304,1152]{1,0:T(8,128)(2,1)} %bitcast.7, bf16[36,112]{1,0:T(8,128)(2,1)} %b_hbm.1), custom_call_target="tpu_custom_call" | custom-call | tf_op jit(solution)/shard_map/half/pallas_call | solution.py:187
  121.6 3.9 %copy.4 = bf16[64,28,896]{2,0,1:T(8,128)(2,1)} copy(bf16[64,28,896]{2,0,1:T(8,128)(2,1)} %bitcast.6) | data formatting | bytes 6422528

commit v3 on v2

v3 whole, which is shorter than its diff:
```python
import jax
import jax.numpy as jnp
from jax import lax
from jax.experimental import pallas as pl
from jax.experimental.pallas import tpu as pltpu
from jax.sharding import PartitionSpec as P

MESH = pl.DeviceIdType.MESH
BF16 = jnp.bfloat16
F32 = jnp.float32
CHUNKS = 14
AHEAD = 4


def one_hot(shape, column_of_row):
    rows = lax.broadcasted_iota(jnp.int32, shape, 0)
    columns = lax.broadcasted_iota(jnp.int32, shape, 1)
    return jnp.where(column_of_row(rows) == columns, 1.0, 0.0).astype(BF16)


def swapped(tile):
    rows = lax.broadcasted_iota(jnp.int32, tile.shape, 0) % 2
    lanes = lax.broadcasted_iota(jnp.int32, tile.shape, 1) // 64
    turned = pltpu.roll(tile, 64, 1)
    above = pltpu.roll(turned, tile.shape[0] - 1, 0)
    below = pltpu.roll(turned, 1, 0)
    return jnp.where(rows == lanes, tile, jnp.where(rows == 0, above, below))


def kernel(
    i_hbm, b_ref, o_ref,
    i_v, b_v, z_v, at_v, g_v, pt_v, perm_v, c_v, s_v, r_v,
    in_sems, zsend, zrecv, gsend, grecv, send_sems, recv_sems,
):
    pq, rs = lax.axis_index("pq"), lax.axis_index("rs")
    zh, x = pq // 4, pq % 4
    y, zl, core = rs // 8, (rs // 2) % 4, rs % 2
    z = zh * 4 + zl

    def column_peer(k):
        pz, pc = (z + k // 2) % 8, (core + k) % 2
        return {"pq": (pz // 4) * 4 + x, "rs": y * 8 + (pz % 4) * 2 + pc}

    def plane_peer(k):
        py, px = (y + k // 4) % 4, (x + k) % 4
        return {"pq": zh * 4 + px, "rs": py * 8 + zl * 2 + core}

    def row_peer(k):
        return {"rs": (rs + k) % 32}

    load_i = pltpu.make_async_copy(i_hbm, i_v, in_sems.at[0])
    load_i.start()
    barrier = pltpu.get_barrier_semaphore()

    def greet(peer):
        def one(k, _):
            pl.semaphore_signal(barrier, inc=1, device_id=peer(k), device_id_type=MESH)
            return 0

        return one

    z_v[...] = jnp.zeros(z_v.shape, BF16)
    b_v[...] = jnp.zeros(b_v.shape, BF16)
    lax.fori_loop(1, 16, greet(column_peer), 0)
    lax.fori_loop(1, 16, greet(plane_peer), 0)
    lax.fori_loop(1, 32, greet(row_peer), 0)

    b_v[:, :, 0:112] = b_ref[...].reshape(9, 4, 112)
    spot = zh * 96 + y * 8 + (zl * 2 + core) * 9
    z_v[pl.ds(spot, 9)] = b_v[...]
    pl.semaphore_wait(barrier, 61)

    def send_block(k, _):
        pltpu.make_async_remote_copy(
            src_ref=b_v, dst_ref=z_v.at[pl.ds(spot, 9)], send_sem=zsend, recv_sem=zrecv,
            device_id=column_peer(k), device_id_type=MESH,
        ).start()
        return 0

    lax.fori_loop(1, 16, send_block, 0)
    order = one_hot((128, 128), lambda n: jnp.where(n < 112, ((n // 2) % 4) * 28 + (n // 8) * 2 + n % 2, -1))
    perm_v[...] = one_hot(
        perm_v.shape, lambda n: ((n // 8) % 8) * 112 + ((n // 2) % 4) * 28 + (n // 64) * 2 + n % 2
    )
    pltpu.make_async_copy(z_v.at[pl.ds(0, 135)], z_v.at[pl.ds(0, 135)], zrecv).wait()
    mine = y * 4 + x

    def spread(q):
        def one(k, _):
            pltpu.make_async_remote_copy(
                src_ref=at_v.at[q], dst_ref=g_v.at[q, mine], send_sem=gsend.at[q], recv_sem=grecv.at[q],
                device_id=plane_peer(k), device_id_type=MESH,
            ).start()
            return 0

        lax.fori_loop(1, 16, one, 0)

    turned = [
        lax.dot_general(
            order, z_v[pl.ds(h * 96, 96)].reshape(384, 128), (((1,), (1,)), ((), ())), preferred_element_type=F32
        ).astype(BF16)
        for h in range(2)
    ]

    def keep(q):
        for h in range(2):
            at_v[q, h] = turned[h][q * 8 : (q + 1) * 8]

    keep(0)
    spread(0)
    for q in range(1, CHUNKS):
        keep(q)
    for q in range(1, AHEAD):
        spread(q)
    g_v[:, mine] = at_v[...]
    load_i.wait()

    def first(q, _):
        pltpu.make_async_copy(g_v.at[q, pl.ds(0, 15)], g_v.at[q, pl.ds(0, 15)], grecv.at[q]).wait()
        rows = pl.ds(pl.multiple_of(q * 64, 64), 64)
        windows = [
            jnp.concatenate([g_v[q, w * 4 + px, h] for h in range(2) for px in range(4)], axis=0) for w in range(4)
        ]
        for t in range(9):
            parts = [windows[w][:, (t - 2 * w) * 128 : (t - 2 * w + 1) * 128] for w in range(4) if 0 <= t - 2 * w < 3]
            pt_v[rows, t * 128 : (t + 1) * 128] = sum(parts[1:], parts[0])

        def columns(u, _):
            for v in range(3):
                g = u * 3 + v
                acc = lax.dot_general(
                    pt_v[rows, :], i_v[pl.ds(pl.multiple_of(g * 256, 256), 256), :], (((1,), (1,)), ((), ())),
                    preferred_element_type=F32,
                )
                for h in range(2):
                    tile = swapped(acc[:, h * 128 : (h + 1) * 128]).astype(BF16)
                    s_v[q, :, 2 * g + h] = tile.reshape(32, 2, 128)
            return 0

        lax.fori_loop(0, 3, columns, 0)

        def issue(k, _):
            d = (rs + k) % 32
            pltpu.make_async_remote_copy(
                src_ref=s_v.at[q, d], dst_ref=r_v.at[q, rs], send_sem=send_sems.at[q], recv_sem=recv_sems.at[q],
                device_id={"rs": d}, device_id_type=MESH,
            ).start()
            return 0

        lax.fori_loop(1, 32, issue, 0)
        r_v[q, rs] = s_v[q, rs]

        @pl.when(q < CHUNKS - AHEAD)
        def _():
            spread(q + AHEAD)

        return 0

    lax.fori_loop(0, CHUNKS, first, 0)

    def natural(g, _):
        rows = pl.ds(pl.multiple_of(g * 128, 128), 128)
        acc = lax.dot_general(pt_v[:, rows], perm_v[...], (((0,), (0,)), ((), ())), preferred_element_type=F32)
        c_v[rows, :] = acc.astype(BF16)
        return 0

    lax.fori_loop(0, 9, natural, 0)

    def second(q, _):
        pltpu.make_async_copy(r_v.at[q, pl.ds(0, 31)], r_v.at[q, pl.ds(0, 31)], recv_sems.at[q]).wait()
        tiles = r_v[q].reshape(NBASIS, 128)
        acc = lax.dot_general(tiles, c_v[...], (((0,), (0,)), ((), ())), preferred_element_type=F32)
        o_ref[q] = acc.astype(BF16)
        return 0

    lax.fori_loop(0, CHUNKS, second, 0)

    def drain(q, _):
        pltpu.make_async_copy(s_v.at[q, pl.ds(0, 31)], s_v.at[q, pl.ds(0, 31)], send_sems.at[q]).wait()
        pltpu.make_async_copy(g_v.at[q, pl.ds(0, 15)], g_v.at[q, pl.ds(0, 15)], gsend.at[q]).wait()
        return 0

    lax.fori_loop(0, CHUNKS, drain, 0)
    pltpu.make_async_copy(z_v.at[pl.ds(0, 135)], z_v.at[pl.ds(0, 135)], zsend).wait()


NBASIS = 1152
NORB = 896


def transform(flat, block):
    far = pl.BlockSpec(memory_space=pltpu.HBM)
    dma = pltpu.SemaphoreType.DMA
    return pl.pallas_call(
        kernel,
        out_shape=jax.ShapeDtypeStruct((CHUNKS, 128, NORB), BF16),
        in_specs=[far, pl.BlockSpec(memory_space=pltpu.VMEM)],
        out_specs=pl.BlockSpec(memory_space=pltpu.VMEM),
        scratch_shapes=[
            pltpu.VMEM((2304, NBASIS), BF16),
            pltpu.VMEM((9, 4, 128), BF16),
            pltpu.VMEM((192, 4, 128), BF16),
            pltpu.VMEM((CHUNKS, 2, 8, 384), BF16),
            pltpu.VMEM((CHUNKS, 16, 2, 8, 384), BF16),
            pltpu.VMEM((NORB, NBASIS), BF16),
            pltpu.VMEM((NORB, NORB), BF16),
            pltpu.VMEM((NBASIS, NORB), BF16),
            pltpu.VMEM((CHUNKS, 32, 18, 2, 128), BF16),
            pltpu.VMEM((CHUNKS, 32, 18, 2, 128), BF16),
            dma((1,)),
            dma,
            dma,
            dma((CHUNKS,)),
            dma((CHUNKS,)),
            dma((CHUNKS,)),
            dma((CHUNKS,)),
        ],
        compiler_params=pltpu.CompilerParams(collective_id=0, has_side_effects=True, vmem_limit_bytes=48 * 2**20),
        name="half",
    )(flat, block)


def on_device(integrals, coeff):
    flat = integrals.transpose(1, 0, 2).reshape(2304, NBASIS)
    return transform(flat, coeff).reshape(28, 64, NORB).transpose(1, 0, 2)


def solution(mesh):
    placed = (P("pq", "rs", None), P("rs", "pq"))
    return jax.shard_map(on_device, mesh=mesh, in_specs=placed, out_specs=P("pq", "rs", None), check_vma=False)
```

time: 126 us -> 120 us (0.952)
  Pallas kernels: 122 us -> 117 us
  local copies, waits for them, and re-layouts: 3.86 us -> 2.39 us
    pallas_call x1, Pallas kernels: 122 us -> 117 us  [transform(): pl.pallas_call(kernel, out_shape=jax.ShapeDtypeStruct((CHUNKS, 128, NORB)...]
    unnamed x1 -> x3, local copies, waits for them, and re-layouts: 3.86 us -> 2.39 us
where the time goes in v3:
time: 120 us
  Pallas kernels  117 us (98%)
  local copies, waits for them, and re-layouts  2.39 us (2%)
    pallas_call x1, Pallas kernels, transform(): pl.pallas_call(kernel, out_shape=jax.ShapeDtypeStruct((CHUNKS, 128, NORB)...  117 us

profile of v3, /device:TPU:1, one launch (start us, length us, event | category | flops | bytes accessed | tf_op | source)
XLA Modules:
  0.0 119.8 jit_solution(4698109104372870848)
XLA Ops:
  0.0 0.0 copy-start
  0.0 0.7 copy-done
  0.7 117.4 %half.1 = bf16[14,128,896]{2,1,0:T(8,128)(2,1)S(1)} custom-call(bf16[2304,1152]{1,0:T(8,128)(2,1)} %bitcast.7, bf16[36,112]{1,0:T(8,128)(2,1)S(1)} %copy-done), custom_call_target="tpu_custom_call" | custom-call | tf_op jit(solution)/shard_map/half/pallas_call | solution.py:194
  118.1 1.7 %copy.4 = bf16[64,28,896]{2,0,1:T(8,128)(2,1)} copy(bf16[64,28,896]{2,0,1:T(8,128)(2,1)S(1)} %bitcast.6) | data formatting | bytes 6422528
Async XLA Ops:
  0.0 0.7 copy-start

commit v4 on v3

v4 whole, which is shorter than its diff:
```python
import functools

import jax
import jax.numpy as jnp
from jax import lax
from jax.experimental import pallas as pl
from jax.experimental.pallas import tpu as pltpu
from jax.sharding import PartitionSpec as P

MESH = pl.DeviceIdType.MESH
BF16 = jnp.bfloat16
F32 = jnp.float32
CHUNKS = 14
DIRECT = 3


def one_hot(shape, column_of_row):
    rows = lax.broadcasted_iota(jnp.int32, shape, 0)
    columns = lax.broadcasted_iota(jnp.int32, shape, 1)
    return jnp.where(column_of_row(rows) == columns, 1.0, 0.0).astype(BF16)


def swapped(tile):
    rows = lax.broadcasted_iota(jnp.int32, tile.shape, 0) % 2
    lanes = lax.broadcasted_iota(jnp.int32, tile.shape, 1) // 64
    turned = pltpu.roll(tile, 64, 1)
    above = pltpu.roll(turned, tile.shape[0] - 1, 0)
    below = pltpu.roll(turned, 1, 0)
    return jnp.where(rows == lanes, tile, jnp.where(rows == 0, above, below))


def kernel(
    i_hbm, b_hbm, o_ref,
    i_v, blk_v, b_v, z_v, at_v, g_v, pt_v, perm_v, c_v, s_v, r_v,
    in_sems, zsend, zrecv, ysend, yrecv, gsend, grecv, send_sems, recv_sems,
):
    pq, rs = lax.axis_index("pq"), lax.axis_index("rs")
    zh, x = pq // 4, pq % 4
    y, zl, core = rs // 8, (rs // 2) % 4, rs % 2
    z = zh * 4 + zl

    def column_peer(k):
        pz, pc = (z + k // 2) % 8, (core + k) % 2
        return {"pq": (pz // 4) * 4 + x, "rs": y * 8 + (pz % 4) * 2 + pc}

    def plane_peer(k):
        py, px = (y + k // 4) % 4, (x + k) % 4
        return {"pq": zh * 4 + px, "rs": py * 8 + zl * 2 + core}

    load_i = pltpu.make_async_copy(i_hbm, i_v, in_sems.at[0])
    load_b = pltpu.make_async_copy(b_hbm, blk_v, in_sems.at[1])
    load_b.start()
    load_i.start()
    barrier = pltpu.get_barrier_semaphore()

    def greet(peer):
        def one(k, _):
            pl.semaphore_signal(barrier, inc=1, device_id=peer(k), device_id_type=MESH)
            return 0

        return one

    z_v[...] = jnp.zeros(z_v.shape, BF16)
    b_v[...] = jnp.zeros(b_v.shape, BF16)
    lax.fori_loop(1, 16, greet(column_peer), 0)
    lax.fori_loop(1, 16, greet(plane_peer), 0)

    load_b.wait()
    b_v[:, :, 0:112] = blk_v[...].reshape(9, 4, 112)
    spot = zh * 96 + y * 8 + (zl * 2 + core) * 9
    z_v[pl.ds(spot, 9)] = b_v[...]
    pl.semaphore_wait(barrier, 30)

    def send_block(n, _):
        k = (n + 7) % 15 + 1
        pltpu.make_async_remote_copy(
            src_ref=b_v, dst_ref=z_v.at[pl.ds(spot, 9)], send_sem=zsend, recv_sem=zrecv,
            device_id=column_peer(k), device_id_type=MESH,
        ).start()
        return 0

    lax.fori_loop(0, 15, send_block, 0)
    order = one_hot((128, 128), lambda n: jnp.where(n < 112, ((n // 2) % 4) * 28 + (n // 8) * 2 + n % 2, -1))
    perm_v[...] = one_hot(
        perm_v.shape, lambda n: ((n // 8) % 8) * 112 + ((n // 2) % 4) * 28 + (n // 64) * 2 + n % 2
    )
    pltpu.make_async_copy(z_v.at[pl.ds(0, 135)], z_v.at[pl.ds(0, 135)], zrecv).wait()
    mine = x * 4 + y

    def spread(q):
        def one(n, _):
            k = (n + 9) % 15 + 1
            pltpu.make_async_remote_copy(
                src_ref=at_v.at[q], dst_ref=g_v.at[q, mine], send_sem=gsend.at[q], recv_sem=grecv.at[q],
                device_id=plane_peer(k), device_id_type=MESH,
            ).start()
            return 0

        lax.fori_loop(0, 15, one, 0)

    strips = [z_v[pl.ds(h * 96, 96)].reshape(384, 128) for h in range(2)]

    def turned(h, rows):
        return lax.dot_general(rows, strips[h], (((1,), (1,)), ((), ())), preferred_element_type=F32).astype(BF16)

    for h in range(2):
        at_v[0, h] = turned(h, order[0:16])[0:8]
    spread(0)
    for h in range(2):
        rest = turned(h, order)
        for q in range(1, CHUNKS):
            at_v[q, h] = rest[q * 8 : (q + 1) * 8]
    for q in range(1, DIRECT):
        spread(q)

    def line(n, _):
        pltpu.make_async_remote_copy(
            src_ref=at_v.at[pl.ds(DIRECT, CHUNKS - DIRECT)], dst_ref=g_v.at[pl.ds(DIRECT, CHUNKS - DIRECT), mine], send_sem=ysend,
            recv_sem=yrecv, device_id={"rs": ((y + 1 + (n + 1) % 3) % 4) * 8 + zl * 2 + core}, device_id_type=MESH,
        ).start()
        return 0

    lax.fori_loop(0, 3, line, 0)
    g_v[:, mine] = at_v[...]
    load_i.wait()

    def across(q, _):
        for n in (2, 1, 3):
            lane = g_v.at[q, pl.ds(x * 4, 4)]
            pltpu.make_async_remote_copy(
                src_ref=lane, dst_ref=lane, send_sem=gsend.at[q], recv_sem=grecv.at[q],
                device_id={"pq": zh * 4 + (x + n) % 4}, device_id_type=MESH,
            ).start()
        return 0

    def arrived(q, blocks, sems):
        pltpu.make_async_copy(g_v.at[q, pl.ds(0, blocks)], g_v.at[q, pl.ds(0, blocks)], sems.at[q]).wait()

    def three_lines(sem):
        every = g_v.at[pl.ds(0, CHUNKS - DIRECT), pl.ds(0, 3)]
        pltpu.make_async_copy(every, every, sem).wait()

    def assemble(q):
        rows = pl.ds(pl.multiple_of(q * 64, 64), 64)
        windows = [
            jnp.concatenate([g_v[q, px * 4 + w, h] for h in range(2) for px in range(4)], axis=0) for w in range(4)
        ]
        for t in range(9):
            parts = [windows[w][:, (t - 2 * w) * 128 : (t - 2 * w + 1) * 128] for w in range(4) if 0 <= t - 2 * w < 3]
            pt_v[rows, t * 128 : (t + 1) * 128] = sum(parts[1:], parts[0])

    def columns(q, u):
        rows = pl.ds(pl.multiple_of(q * 64, 64), 64)
        for v in range(3):
            g = u * 3 + v
            acc = lax.dot_general(
                pt_v[rows, :], i_v[pl.ds(pl.multiple_of(g * 256, 256), 256), :], (((1,), (1,)), ((), ())),
                preferred_element_type=F32,
            )
            for h in range(2):
                tile = swapped(acc[:, h * 128 : (h + 1) * 128]).astype(BF16)
                s_v[q, :, 2 * g + h] = tile.reshape(32, 2, 128)

    def exchange(q, start, size):
        part = pl.ds(start, size)

        def issue(k, _):
            d = (rs + k) % 32
            pltpu.make_async_remote_copy(
                src_ref=s_v.at[q, d, part], dst_ref=r_v.at[q, rs, part], send_sem=send_sems.at[q],
                recv_sem=recv_sems.at[q], device_id={"rs": d}, device_id_type=MESH,
            ).start()
            return 0

        lax.fori_loop(1, 32, issue, 0)

    arrived(0, 15, grecv)
    assemble(0)
    for u in range(3):
        columns(0, u)
        exchange(0, u * 6, 6)
    r_v[0, rs] = s_v[0, rs]

    def first(blocks, q, _):
        arrived(q, blocks, grecv)
        assemble(q)

        def some(u, _):
            columns(q, u)
            return 0

        lax.fori_loop(0, 3, some, 0)
        exchange(q, 0, 18)
        r_v[q, rs] = s_v[q, rs]
        return 0

    lax.fori_loop(1, DIRECT, functools.partial(first, 15), 0)
    three_lines(yrecv)
    lax.fori_loop(DIRECT, CHUNKS, across, 0)
    lax.fori_loop(DIRECT, CHUNKS, functools.partial(first, 12), 0)

    def natural(g, _):
        rows = pl.ds(pl.multiple_of(g * 128, 128), 128)
        acc = lax.dot_general(pt_v[:, rows], perm_v[...], (((0,), (0,)), ((), ())), preferred_element_type=F32)
        c_v[rows, :] = acc.astype(BF16)
        return 0

    lax.fori_loop(0, 9, natural, 0)

    def second(q, _):
        pltpu.make_async_copy(r_v.at[q, pl.ds(0, 31)], r_v.at[q, pl.ds(0, 31)], recv_sems.at[q]).wait()
        tiles = r_v[q].reshape(NBASIS, 128)
        acc = lax.dot_general(tiles, c_v[...], (((0,), (0,)), ((), ())), preferred_element_type=F32)
        o_ref[q] = acc.astype(BF16)
        return 0

    lax.fori_loop(0, CHUNKS, second, 0)

    def drain(q, _):
        pltpu.make_async_copy(s_v.at[q, pl.ds(0, 31)], s_v.at[q, pl.ds(0, 31)], send_sems.at[q]).wait()
        return 0

    lax.fori_loop(0, CHUNKS, drain, 0)
    for q in range(CHUNKS):
        arrived(q, 15 if q < DIRECT else 12, gsend)
    three_lines(ysend)
    pltpu.make_async_copy(z_v.at[pl.ds(0, 135)], z_v.at[pl.ds(0, 135)], zsend).wait()


NBASIS = 1152
NORB = 896


def transform(flat, block):
    far = pl.BlockSpec(memory_space=pltpu.HBM)
    dma = pltpu.SemaphoreType.DMA
    return pl.pallas_call(
        kernel,
        out_shape=jax.ShapeDtypeStruct((CHUNKS, 128, NORB), BF16),
        in_specs=[far, far],
        out_specs=pl.BlockSpec(memory_space=pltpu.VMEM),
        scratch_shapes=[
            pltpu.VMEM((2304, NBASIS), BF16),
            pltpu.VMEM((36, 112), BF16),
            pltpu.VMEM((9, 4, 128), BF16),
            pltpu.VMEM((192, 4, 128), BF16),
            pltpu.VMEM((CHUNKS, 2, 8, 384), BF16),
            pltpu.VMEM((CHUNKS, 16, 2, 8, 384), BF16),
            pltpu.VMEM((NORB, NBASIS), BF16),
            pltpu.VMEM((NORB, NORB), BF16),
            pltpu.VMEM((NBASIS, NORB), BF16),
            pltpu.VMEM((CHUNKS, 32, 18, 2, 128), BF16),
            pltpu.VMEM((CHUNKS, 32, 18, 2, 128), BF16),
            dma((2,)),
            dma,
            dma,
            dma,
            dma,
            dma((CHUNKS,)),
            dma((CHUNKS,)),
            dma((CHUNKS,)),
            dma((CHUNKS,)),
        ],
        compiler_params=pltpu.CompilerParams(collective_id=0, has_side_effects=True, vmem_limit_bytes=48 * 2**20),
        name="half",
    )(flat, block)


def on_device(integrals, coeff):
    flat = integrals.transpose(1, 0, 2).reshape(2304, NBASIS)
    return transform(flat, pltpu.with_memory_space_constraint(coeff, pltpu.HBM)).reshape(28, 64, NORB).transpose(1, 0, 2)


def solution(mesh):
    placed = (P("pq", "rs", None), P("rs", "pq"))
    return jax.shard_map(on_device, mesh=mesh, in_specs=placed, out_specs=P("pq", "rs", None), check_vma=False)
```

time: 120 us -> 117 us (0.975)
    pallas_call x1, Pallas kernels: 117 us -> 116 us  [transform(): pl.pallas_call(kernel, out_shape=jax.ShapeDtypeStruct((CHUNKS, 128, NORB)...]
where the time goes in v4:
time: 117 us
  Pallas kernels  116 us (99%)
  local copies, waits for them, and re-layouts  1.69 us (1%)
    pallas_call x1, Pallas kernels, transform(): pl.pallas_call(kernel, out_shape=jax.ShapeDtypeStruct((CHUNKS, 128, NORB)...  116 us

profile of v4, /device:TPU:1, one launch (start us, length us, event | category | flops | bytes accessed | tf_op | source)
XLA Modules:
  0.0 117.3 jit_solution(9198735360447947)
XLA Ops:
  0.0 115.6 %half.1 = bf16[14,128,896]{2,1,0:T(8,128)(2,1)S(1)} custom-call(bf16[2304,1152]{1,0:T(8,128)(2,1)} %bitcast.7, bf16[36,112]{1,0:T(8,128)(2,1)} %b_hbm.1), custom_call_target="tpu_custom_call" | custom-call | tf_op jit(solution)/shard_map/half/pallas_call | solution.py:237
  115.6 1.7 %copy.4 = bf16[64,28,896]{2,0,1:T(8,128)(2,1)} copy(bf16[64,28,896]{2,0,1:T(8,128)(2,1)S(1)} %bitcast.6) | data formatting | bytes 6422528

commit v5 on v4

--- a/solution.py
+++ b/solution.py
@@ -62,8 +62,8 @@
 
     z_v[...] = jnp.zeros(z_v.shape, BF16)
     b_v[...] = jnp.zeros(b_v.shape, BF16)
-    lax.fori_loop(1, 16, greet(column_peer), 0)
-    lax.fori_loop(1, 16, greet(plane_peer), 0)
+    lax.fori_loop(1, 16, greet(column_peer), 0, unroll=True)
+    lax.fori_loop(1, 16, greet(plane_peer), 0, unroll=True)
 
     load_b.wait()
     b_v[:, :, 0:112] = blk_v[...].reshape(9, 4, 112)
@@ -79,7 +79,7 @@
         ).start()
         return 0
 
-    lax.fori_loop(0, 15, send_block, 0)
+    lax.fori_loop(0, 15, send_block, 0, unroll=True)
     order = one_hot((128, 128), lambda n: jnp.where(n < 112, ((n // 2) % 4) * 28 + (n // 8) * 2 + n % 2, -1))
     perm_v[...] = one_hot(
         perm_v.shape, lambda n: ((n // 8) % 8) * 112 + ((n // 2) % 4) * 28 + (n // 64) * 2 + n % 2
@@ -96,7 +96,7 @@
             ).start()
             return 0
 
-        lax.fori_loop(0, 15, one, 0)
+        lax.fori_loop(0, 15, one, 0, unroll=True)
 
     strips = [z_v[pl.ds(h * 96, 96)].reshape(384, 128) for h in range(2)]
 
@@ -165,14 +165,14 @@
         part = pl.ds(start, size)
 
         def issue(k, _):
-            d = (rs + k) % 32
+            d = (rs + k + core * (32 - 2 * k)) % 32
             pltpu.make_async_remote_copy(
                 src_ref=s_v.at[q, d, part], dst_ref=r_v.at[q, rs, part], send_sem=send_sems.at[q],
                 recv_sem=recv_sems.at[q], device_id={"rs": d}, device_id_type=MESH,
             ).start()
             return 0
 
-        lax.fori_loop(1, 32, issue, 0)
+        lax.fori_loop(1, 32, issue, 0, unroll=size < 18)
 
     arrived(0, 15, grecv)
     assemble(0)

time: 117 us -> 117 us (level)
  no operation moved by 1% of the time
where the time goes in v5:
time: 117 us
  Pallas kernels  115 us (98%)
  local copies, waits for them, and re-layouts  1.69 us (1%)
    pallas_call x1, Pallas kernels, transform(): pl.pallas_call(kernel, out_shape=jax.ShapeDtypeStruct((CHUNKS, 128, NORB)...  115 us

profile of v5, /device:TPU:1, one launch (start us, length us, event | category | flops | bytes accessed | tf_op | source)
XLA Modules:
  0.0 116.8 jit_solution(3878036751715115220)
XLA Ops:
  0.0 115.1 %half.1 = bf16[14,128,896]{2,1,0:T(8,128)(2,1)S(1)} custom-call(bf16[2304,1152]{1,0:T(8,128)(2,1)} %bitcast.7, bf16[36,112]{1,0:T(8,128)(2,1)} %b_hbm.1), custom_call_target="tpu_custom_call" | custom-call | tf_op jit(solution)/shard_map/half/pallas_call | solution.py:237
  115.1 1.7 %copy.4 = bf16[64,28,896]{2,0,1:T(8,128)(2,1)} copy(bf16[64,28,896]{2,0,1:T(8,128)(2,1)S(1)} %bitcast.6) | data formatting | bytes 6422528

commit v6 on v5

--- a/solution.py
+++ b/solution.py
@@ -206,6 +206,10 @@
         return 0
 
     lax.fori_loop(0, 9, natural, 0)
+    for q in range(CHUNKS):
+        arrived(q, 15 if q < DIRECT else 12, gsend)
+    three_lines(ysend)
+    pltpu.make_async_copy(z_v.at[pl.ds(0, 135)], z_v.at[pl.ds(0, 135)], zsend).wait()
 
     def second(q, _):
         pltpu.make_async_copy(r_v.at[q, pl.ds(0, 31)], r_v.at[q, pl.ds(0, 31)], recv_sems.at[q]).wait()
@@ -214,17 +218,14 @@
         o_ref[q] = acc.astype(BF16)
         return 0
 
-    lax.fori_loop(0, CHUNKS, second, 0)
-
     def drain(q, _):
         pltpu.make_async_copy(s_v.at[q, pl.ds(0, 31)], s_v.at[q, pl.ds(0, 31)], send_sems.at[q]).wait()
         return 0
 
-    lax.fori_loop(0, CHUNKS, drain, 0)
-    for q in range(CHUNKS):
-        arrived(q, 15 if q < DIRECT else 12, gsend)
-    three_lines(ysend)
-    pltpu.make_async_copy(z_v.at[pl.ds(0, 135)], z_v.at[pl.ds(0, 135)], zsend).wait()
+    lax.fori_loop(0, CHUNKS - 1, second, 0)
+    lax.fori_loop(0, CHUNKS - 1, drain, 0)
+    second(CHUNKS - 1, 0)
+    drain(CHUNKS - 1, 0)
 
 
 NBASIS = 1152

time: 117 us -> 117 us (level)
  no operation moved by 1% of the time
where the time goes in v6:
time: 117 us
  Pallas kernels  115 us (98%)
  local copies, waits for them, and re-layouts  1.69 us (1%)
    pallas_call x1, Pallas kernels, transform(): pl.pallas_call(kernel, out_shape=jax.ShapeDtypeStruct((CHUNKS, 128, NORB)...  115 us

profile of v6, /device:TPU:1, one launch (start us, length us, event | category | flops | bytes accessed | tf_op | source)
XLA Modules:
  0.0 116.6 jit_solution(7549111168169237593)
XLA Ops:
  0.0 115.0 %half.1 = bf16[14,128,896]{2,1,0:T(8,128)(2,1)S(1)} custom-call(bf16[2304,1152]{1,0:T(8,128)(2,1)} %bitcast.7, bf16[36,112]{1,0:T(8,128)(2,1)} %b_hbm.1), custom_call_target="tpu_custom_call" | custom-call | tf_op jit(solution)/shard_map/half/pallas_call | solution.py:238
  115.0 1.7 %copy.4 = bf16[64,28,896]{2,0,1:T(8,128)(2,1)} copy(bf16[64,28,896]{2,0,1:T(8,128)(2,1)S(1)} %bitcast.6) | data formatting | bytes 6422528

commit v7 on v6

--- a/solution.py
+++ b/solution.py
@@ -149,10 +149,10 @@
             parts = [windows[w][:, (t - 2 * w) * 128 : (t - 2 * w + 1) * 128] for w in range(4) if 0 <= t - 2 * w < 3]
             pt_v[rows, t * 128 : (t + 1) * 128] = sum(parts[1:], parts[0])
 
-    def columns(q, u):
+    def columns(q, first_group, groups):
         rows = pl.ds(pl.multiple_of(q * 64, 64), 64)
-        for v in range(3):
-            g = u * 3 + v
+        for v in range(groups):
+            g = first_group + v
             acc = lax.dot_general(
                 pt_v[rows, :], i_v[pl.ds(pl.multiple_of(g * 256, 256), 256), :], (((1,), (1,)), ((), ())),
                 preferred_element_type=F32,
@@ -176,9 +176,9 @@
 
     arrived(0, 15, grecv)
     assemble(0)
-    for u in range(3):
-        columns(0, u)
-        exchange(0, u * 6, 6)
+    for start, size in ((0, 2), (2, 3), (5, 4)):
+        columns(0, start, size)
+        exchange(0, start * 2, size * 2)
     r_v[0, rs] = s_v[0, rs]
 
     def first(blocks, q, _):
@@ -186,7 +186,7 @@
         assemble(q)
 
         def some(u, _):
-            columns(q, u)
+            columns(q, u * 3, 3)
             return 0
 
         lax.fori_loop(0, 3, some, 0)

time: 117 us -> 117 us (level)
  no operation moved by 1% of the time
where the time goes in v7:
time: 117 us
  Pallas kernels  115 us (98%)
  local copies, waits for them, and re-layouts  1.69 us (1%)
    pallas_call x1, Pallas kernels, transform(): pl.pallas_call(kernel, out_shape=jax.ShapeDtypeStruct((CHUNKS, 128, NORB)...  115 us

profile of v7, /device:TPU:1, one launch (start us, length us, event | category | flops | bytes accessed | tf_op | source)
XLA Modules:
  0.0 116.9 jit_solution(17815531352952508563)
XLA Ops:
  0.0 115.3 %half.1 = bf16[14,128,896]{2,1,0:T(8,128)(2,1)S(1)} custom-call(bf16[2304,1152]{1,0:T(8,128)(2,1)} %bitcast.7, bf16[36,112]{1,0:T(8,128)(2,1)} %b_hbm.1), custom_call_target="tpu_custom_call" | custom-call | tf_op jit(solution)/shard_map/half/pallas_call | solution.py:238
  115.3 1.7 %copy.4 = bf16[64,28,896]{2,0,1:T(8,128)(2,1)} copy(bf16[64,28,896]{2,0,1:T(8,128)(2,1)S(1)} %bitcast.6) | data formatting | bytes 6422528
